TPU v7x, 32 devices: a whole 2x2x4 slice. The times are simulated.
32 devices in a mesh: seq: 4 (over x, core), vocab: 8 (over z, y).
Axes of the slice: x: 2, y: 2, z: 4, core: 2. Of those that a mesh axis runs over, the one named last changes fastest.
Arguments:
- hidden: bfloat16 [512, 4608], P('seq', 'vocab'), may hold values from -6 to 6
- norm_gain: float32 [4608], replicated, may hold values from -1.5 to 1.5
- unembed: bfloat16 [256000, 4608], P(('seq', 'vocab')), may hold values from -0.375 to 0.375
- targets: int32 [512], P('seq'), may hold values from 0 to 255999
Outputs:
- log_prob: float32 [512], P('seq')
- entropy: float32 [512], P('seq')
All inputs are finite; a program needn't handle non-finite values.
Results may differ from a plain program's by a relative error of at most 0.0012.
Values may be sent and summed in bfloat16 or wider, within the bound.
A program may use at most 128 MiB of HBM per device.

v0:
```python
import jax
import jax.numpy as jnp
from jax import lax
from jax.sharding import PartitionSpec as P

softcap = 30.0
epsilon = 1e-06


def token_stats(logits, target_rows, first):
    capped = softcap * jnp.tanh(logits / softcap)
    weights = jnp.exp(capped - softcap)
    columns = first + lax.broadcasted_iota(jnp.int32, logits.shape, 1)
    chosen = jnp.where(columns == target_rows[:, None], capped, 0.0)
    return jnp.stack(
        [jnp.sum(weights, axis=1), jnp.sum(weights * capped, axis=1), jnp.sum(chosen, axis=1)]
    )


def on_device(hidden, norm_gain, unembed, targets):
    vocab_rows = unembed.shape[0]
    own_tokens = hidden.shape[0]
    first = lax.axis_index(("seq", "vocab")) * vocab_rows
    all_targets = lax.all_gather(targets, "seq", axis=0, tiled=True)
    rows = lax.all_gather(hidden, "vocab", axis=1, tiled=True).astype(jnp.float32)
    scale = lax.rsqrt(jnp.mean(rows * rows, axis=1, keepdims=True) + epsilon)
    normed = (rows * scale * (1.0 + norm_gain)).astype(jnp.bfloat16)
    logits = lax.dot_general(
        lax.all_gather(normed, "seq", axis=0, tiled=True),
        unembed,
        (((1,), (1,)), ((), ())),
        preferred_element_type=jnp.float32,
    )
    stats = token_stats(logits, all_targets, first)
    summed = lax.psum(stats, ("seq", "vocab"))
    mine = lax.dynamic_slice_in_dim(summed, lax.axis_index("seq") * own_tokens, own_tokens, 1)
    total = mine[0]
    moment = mine[1]
    chosen = mine[2]
    log_norm = softcap + jnp.log(total)
    return (chosen - log_norm, log_norm - moment / total)


def solution(mesh):
    return jax.shard_map(
        on_device,
        mesh=mesh,
        in_specs=(P("seq", "vocab"), P(), P(("seq", "vocab"), None), P("seq")),
        out_specs=(P("seq"), P("seq")),
        check_vma=False,
    )
```

profile of v0, /device:TPU:0, one launch (start us, length us, event | category | flops | bytes accessed | tf_op | source)
XLA Modules:
  0.0 194.3 jit_solution(5912990735798231276)
XLA Ops:
  7.2 0.0 all-gather.4.cloned.1.call-start
  7.2 0.7 all-gather.4.cloned.1.call-update
  7.9 0.0 all-gather.6.cloned.1.call-start
  7.9 0.7 broadcast_add_fusion
  8.7 45.4 %all-gather.4.cloned.1.call-done = bf16[128,4608]{0,1:T(8,128)(2,1)} async-done(((bf16[128,576]{0,1:T(8,128)(2,1)}), bf16[128,4608]{0,1:T(8,128)(2,1)}) %all-gather.4.cloned.1.call-update) | async-done | bytes 1179664 | tf_op jit(solution)/shard_map/all_gather | solution.py:25
  54.0 1.9 fusion.1
  55.9 3.9 %fusion.3 = bf16[128,4608]{0,1:T(8,128)(2,1)} fusion(bf16[128,4608]{0,1:T(8,128)(2,1)} %all-gather.4.cloned.1.call-done, f32[4608]{0:T(1024)S(1)} %broadcast_add_fusion, f32[128]{0:T(128)S(1)} %add_rsqrt_fusion), kind=kLoop, calls=%fused_computation.9 | loop fusion | flops 2359296 | bytes 2378240 | tf_op jit(solution)/shard_map/convert_element_type | solution.py:27
  59.8 0.0 all-gather.6.cloned.1.call-update
  59.8 5.2 %all-gather = s32[4,1,128]{2,1,0:T(1,128)S(1)} all-gather(s32[1,1,128]{2,1,0:T(1,128)} %bitcast.15), channel_id=1, replica_groups=mesh['seq'=4,'vocab'=8] {'seq'}, dimensions={0}, use_global_device_ids=true | all-gather | bytes 2560 | tf_op jit(solution)/shard_map/all_gather | solution.py:24
  65.0 31.7 %all-gather.6.cloned.1.call-done = bf16[512,4608]{0,1:T(8,128)(2,1)} async-done(((bf16[128,4608]{0,1:T(8,128)(2,1)}), bf16[512,4608]{0,1:T(8,128)(2,1)}) %all-gather.6.cloned.1.call-update) | async-done | bytes 4718608 | tf_op jit(solution)/shard_map/all_gather | solution.py:29
  96.7 50.8 %fusion = (f32[512]{0:T(512)S(1)}, f32[512]{0:T(512)S(1)}, f32[512]{0:T(512)S(1)}) fusion(s32[512]{0:T(512)S(1)} %bitcast.14, s32[8000]{0:T(1024)S(1)} %iota_add_fusion, bf16[8000,4608]{1,0:T(8,128)(2,1)} %param.6, bf16[512,4608]{0,1:T(8,128)(2,1)} %all-gather.6.cloned.1.call-done), kind=kOutput, calls=%fused_computation.3 | convolution fusion | flops 37785600000 | bytes 78486784 | tf_op jit(solution)/shard_map/dot_general | solution.py:28
  147.6 39.4 %psum.7 = f32[3,512]{1,0:T(4,128)S(1)} all-reduce(f32[3,512]{1,0:T(4,128)S(1)} %pad_maximum_fusion), channel_id=1, replica_groups=mesh['seq'=4,'vocab'=8] {'seq','vocab'}, use_global_device_ids=true, to_apply=%region_4.5 | all-reduce | flops 1536 | bytes 12288 | tf_op jit(solution)/shard_map/psum | solution.py:35
  186.9 0.5 subtract_bitcast_fusion
  (4 shorter events, 0.0 us)
Async XLA Ops:
  7.2 46.9 %all-gather.4.cloned.1.call-start = ((), (), s32[]{:S(2)}) async-start(), calls=%async_computation | async-start | bytes 1327104 | tf_op jit(solution)/shard_map/all_gather | solution.py:25
  7.9 88.8 %all-gather.6.cloned.1.call-start = ((), (), s32[]{:S(2)}) async-start(), calls=%async_computation.1 | async-start | bytes 5898240 | tf_op jit(solution)/shard_map/all_gather | solution.py:29
Sparse Core Ops, SparseCore 0:
  10.2 43.8 all-gather.3
  59.9 36.7 all-gather.5
where the time goes:
time: 195 us; the launch traced here: 194 us
  waiting for transfers between devices  77.7 us (40%)
  matrix products  50.8 us (26%)
  blocking collectives  44.6 us (23%)
  between operations  14.1 us (7%)
  other arithmetic  7.03 us (4%)
    dot_general x1, matrix products, on_device(): lax.dot_general(lax.all_gather(normed, 'seq', axis=0, tiled=True), unembe...  50.8 us
    all_gather x1, waiting for transfers between devices, on_device(): lax.all_gather(hidden, 'vocab', axis=1, tiled=True).astype(jnp.float32)  45.4 us
    psum x1, blocking collectives, on_device(): summed = lax.psum(stats, ('seq', 'vocab'))  39.4 us
    all_gather x1, waiting for transfers between devices, on_device(): lax.all_gather(normed, 'seq', axis=0, tiled=True)  31.7 us
    all_gather x1, blocking collectives, on_device(): all_targets = lax.all_gather(targets, 'seq', axis=0, tiled=True)  5.2 us
  transfers between devices with their start and end apart: 2, of which 2 were waited for; matrix products, arithmetic and copies ran while one was open for 0% of the time, Pallas kernels for 0%

commit v1 on v0

--- a/solution.py
+++ b/solution.py
@@ -32,7 +32,7 @@
         preferred_element_type=jnp.float32,
     )
     stats = token_stats(logits, all_targets, first)
-    summed = lax.psum(stats, ("seq", "vocab"))
+    summed = lax.psum(lax.psum(stats, "vocab"), "seq")
     mine = lax.dynamic_slice_in_dim(summed, lax.axis_index("seq") * own_tokens, own_tokens, 1)
     total = mine[0]
     moment = mine[1]

time: 195 us -> 183 us (0.938)
  blocking collectives: 44.6 us -> 32.9 us
    psum x1 -> x2, blocking collectives: 39.4 us -> 27.7 us  [on_device(): summed = lax.psum(lax.psum(stats, 'vocab'), 'seq')]
where the time goes in v1:
time: 183 us
  waiting for transfers between devices  77.7 us (42%)
  matrix products  50.8 us (28%)
  blocking collectives  32.9 us (18%)
  between operations  14.1 us (8%)
  other arithmetic  7.03 us (4%)
    dot_general x1, matrix products, on_device(): lax.dot_general(lax.all_gather(normed, 'seq', axis=0, tiled=True), unembe...  50.8 us
    all_gather x1, waiting for transfers between devices, on_device(): lax.all_gather(hidden, 'vocab', axis=1, tiled=True).astype(jnp.float32)  45.4 us
    all_gather x1, waiting for transfers between devices, on_device(): lax.all_gather(normed, 'seq', axis=0, tiled=True)  31.7 us
    psum x2, blocking collectives, on_device(): summed = lax.psum(lax.psum(stats, 'vocab'), 'seq')  27.7 us
    all_gather x1, blocking collectives, on_device(): all_targets = lax.all_gather(targets, 'seq', axis=0, tiled=True)  5.2 us
    convert_element_type x1, other arithmetic, on_device(): normed = (rows * scale * (1.0 + norm_gain)).astype(jnp.bfloat16)  3.85 us
  transfers between devices with their start and end apart: 2, of which 2 were waited for; matrix products, arithmetic and copies ran while one was open for 0% of the time, Pallas kernels for 0%

profile of v1, /device:TPU:0, one launch (start us, length us, event | category | flops | bytes accessed | tf_op | source)
XLA Modules:
  0.0 182.7 jit_solution(4877591059456979763)
XLA Ops:
  7.2 0.0 all-gather.4.cloned.1.call-start
  7.2 0.7 all-gather.4.cloned.1.call-update
  7.9 0.0 all-gather.6.cloned.1.call-start
  7.9 0.7 broadcast_add_fusion
  8.7 45.4 %all-gather.4.cloned.1.call-done = bf16[128,4608]{0,1:T(8,128)(2,1)} async-done(((bf16[128,576]{0,1:T(8,128)(2,1)}), bf16[128,4608]{0,1:T(8,128)(2,1)}) %all-gather.4.cloned.1.call-update) | async-done | bytes 1179664 | tf_op jit(solution)/shard_map/all_gather | solution.py:25
  54.0 1.9 %fusion.1 = f32[128]{0:T(128)S(1)} fusion(bf16[128,4608]{0,1:T(8,128)(2,1)} %all-gather.4.cloned.1.call-done), kind=kLoop, calls=%fused_computation.7 | loop fusion | flops 1769344 | bytes 1180160 | tf_op jit(solution)/shard_map/reduce_sum | solution.py:26
  55.9 3.9 %fusion.3 = bf16[128,4608]{0,1:T(8,128)(2,1)} fusion(bf16[128,4608]{0,1:T(8,128)(2,1)} %all-gather.4.cloned.1.call-done, f32[4608]{0:T(1024)S(1)} %broadcast_add_fusion, f32[128]{0:T(128)S(1)} %add_rsqrt_fusion), kind=kLoop, calls=%fused_computation.9 | loop fusion | flops 2359296 | bytes 2378240 | tf_op jit(solution)/shard_map/convert_element_type | solution.py:27
  59.8 0.0 all-gather.6.cloned.1.call-update
  59.8 5.2 %all-gather = s32[4,1,128]{2,1,0:T(1,128)S(1)} all-gather(s32[1,1,128]{2,1,0:T(1,128)} %bitcast.15), channel_id=1, replica_groups=mesh['seq'=4,'vocab'=8] {'seq'}, dimensions={0}, use_global_device_ids=true | all-gather | bytes 2560 | tf_op jit(solution)/shard_map/all_gather | solution.py:24
  65.0 31.7 %all-gather.6.cloned.1.call-done = bf16[512,4608]{0,1:T(8,128)(2,1)} async-done(((bf16[128,4608]{0,1:T(8,128)(2,1)}), bf16[512,4608]{0,1:T(8,128)(2,1)}) %all-gather.6.cloned.1.call-update) | async-done | bytes 4718608 | tf_op jit(solution)/shard_map/all_gather | solution.py:29
  96.7 50.8 %fusion = (f32[512]{0:T(512)S(1)}, f32[512]{0:T(512)S(1)}, f32[512]{0:T(512)S(1)}) fusion(s32[512]{0:T(512)S(1)} %bitcast.14, s32[8000]{0:T(1024)S(1)} %iota_add_fusion, bf16[8000,4608]{1,0:T(8,128)(2,1)} %param.6, bf16[512,4608]{0,1:T(8,128)(2,1)} %all-gather.6.cloned.1.call-done), kind=kOutput, calls=%fused_computation.3 | convolution fusion | flops 37785600000 | bytes 78486784 | tf_op jit(solution)/shard_map/dot_general | solution.py:28
  147.6 21.6 %psum.14 = f32[3,512]{1,0:T(4,128)S(1)} all-reduce(f32[3,512]{1,0:T(4,128)S(1)} %pad_maximum_fusion), channel_id=1, replica_groups=mesh['seq'=4,'vocab'=8] {'vocab'}, use_global_device_ids=true, to_apply=%region_4.5 | all-reduce | flops 1536 | bytes 12288 | tf_op jit(solution)/shard_map/psum | solution.py:35
  169.2 6.1 %psum.15 = f32[3,512]{1,0:T(4,128)S(1)} all-reduce(f32[3,512]{1,0:T(4,128)S(1)} %psum.14), channel_id=1, replica_groups=mesh['seq'=4,'vocab'=8] {'seq'}, use_global_device_ids=true, to_apply=%region_5.6 | all-reduce | flops 1536 | bytes 12288 | tf_op jit(solution)/shard_map/psum | solution.py:35
  175.3 0.5 subtract_bitcast_fusion
  (4 shorter events, 0.0 us)
Async XLA Ops:
  7.2 46.9 %all-gather.4.cloned.1.call-start = ((), (), s32[]{:S(2)}) async-start(), calls=%async_computation | async-start | bytes 1327104 | tf_op jit(solution)/shard_map/all_gather | solution.py:25
  7.9 88.8 %all-gather.6.cloned.1.call-start = ((), (), s32[]{:S(2)}) async-start(), calls=%async_computation.1 | async-start | bytes 5898240 | tf_op jit(solution)/shard_map/all_gather | solution.py:29
Sparse Core Ops, SparseCore 0:
  10.2 43.8 all-gather.3
  59.9 36.7 all-gather.5
